TPU v7x, 32 devices: a whole 2x2x4 slice. The times are simulated.
32 devices in a mesh: rep: 2 (over y), span: 2 (over core), seq: 4 (over z), tp: 2 (over x).
Axes of the slice: x: 2, y: 2, z: 4, core: 2. Of those that a mesh axis runs over, the one named last changes fastest.
Arguments:
- queries: bfloat16 [8, 512, 24, 128], P(('rep', 'span'), 'seq', 'tp'), parts along dimension 0, may hold values from -110 to 110
- key_states: bfloat16 [8, 512, 4, 128], P(('rep', 'span'), 'seq', 'tp'), parts along dimension 0, may hold values from -11 to 11
- value_states: bfloat16 [8, 512, 4, 128], P(('rep', 'span'), 'seq', 'tp'), parts along dimension 0, may hold values from -6 to 6
- out_weight: bfloat16 [3072, 6144], P('tp', 'seq'), may hold values from -0.109375 to 0.109375
- noise_table: float32 [64, 6144], P(None, 'tp'), may hold values from 0.5 to 2
- plan: int32 [8], P('rep'), parts along dimension 0, may hold values from 0 to 63
Outputs:
- branch_out: bfloat16 [8, 512, 6144], P(('rep', 'span'), 'seq', 'tp'), parts along dimension 0
There are 2 independent parts, one for each index of `rep`. A program takes and returns all parts, laid end to end along the dimension named above; an argument that names none is the same for every part. Nothing has to cross between parts.
All inputs are finite; a program needn't handle non-finite values.
Results may differ from a plain program's by a relative error of at most 0.014.
Values may be sent and summed in bfloat16 or wider, within the bound.
A program may use at most 128 MiB of HBM per device.

v0:
```python
import jax
import jax.numpy as jnp
from jax import lax
from jax.sharding import PartitionSpec as P


def fold_block(carried, query_rows, key_rows, value_rows, factor):
    maxima, totals, weighted = carried
    scores = (
        jnp.einsum("tkgd,skd->tkgs", query_rows, key_rows, preferred_element_type=jnp.float32)
        * factor
    )
    highest = jnp.maximum(maxima, jnp.max(scores, axis=-1))
    shrink = jnp.exp(maxima - highest)
    weights = jnp.exp(scores - highest[..., None])
    totals = totals * shrink + jnp.sum(weights, axis=-1)
    weighted = weighted * shrink[..., None] + jnp.einsum(
        "tkgs,skd->tkgd",
        weights.astype(jnp.bfloat16),
        value_rows,
        preferred_element_type=jnp.float32,
    )
    return (maxima * 0.0 + highest, totals, weighted)


def per_device(queries, key_states, value_states, out_weight, noise_table, plan):
    ch_dev, tok_dev, heads_local, head_size = queries.shape
    kv_local = key_states.shape[2]
    per_kv = heads_local // kv_local
    span_count = ch_dev * lax.axis_size("span")
    first_span = lax.axis_index("span") * ch_dev
    factor = head_size ** (-0.5)
    grouped = queries.reshape(ch_dev, tok_dev, kv_local, per_kv, head_size)
    start_max = jnp.full((ch_dev, tok_dev, kv_local, per_kv), -1e30, jnp.float32)
    start_tot = jnp.zeros((ch_dev, tok_dev, kv_local, per_kv), jnp.float32)
    start_acc = jnp.zeros((ch_dev, tok_dev, kv_local, per_kv, head_size), jnp.float32)
    span_rows = (
        lax.all_gather(key_states, "seq", axis=1, tiled=True),
        lax.all_gather(value_states, "seq", axis=1, tiled=True),
    )
    key_piece = lax.all_gather(span_rows[0], "span", axis=0, tiled=True)
    value_piece = lax.all_gather(span_rows[1], "span", axis=0, tiled=True)
    new_max = []
    new_tot = []
    new_acc = []
    for q_span in range(ch_dev):
        inner_state = (start_max[q_span], start_tot[q_span], start_acc[q_span])
        for k_span in range(span_count):

            def update(inner, q_span=q_span, k_span=k_span):
                return fold_block(
                    inner, grouped[q_span], key_piece[k_span], value_piece[k_span], factor
                )

            inner_state = lax.cond(
                k_span <= first_span + q_span, update, lambda inner: inner, inner_state
            )
        new_max.append(inner_state[0])
        new_tot.append(inner_state[1])
        new_acc.append(inner_state[2])
    attn = (
        (jnp.stack(new_acc) / jnp.stack(new_tot)[..., None])
        .reshape(ch_dev, tok_dev, heads_local * head_size)
        .astype(jnp.bfloat16)
    )
    columns = jnp.einsum(
        "ctf,fo->cto",
        lax.all_gather(attn, "seq", axis=1, tiled=True),
        out_weight,
        preferred_element_type=jnp.float32,
    )
    partial_out = lax.all_to_all(
        columns.astype(jnp.bfloat16), "seq", split_axis=1, concat_axis=2, tiled=True
    ).astype(columns.dtype)
    summed = lax.psum_scatter(
        partial_out.astype(jnp.bfloat16), "tp", scatter_dimension=2, tiled=True
    ).astype(jnp.float32)
    levels = lax.dynamic_slice_in_dim(plan, first_span, ch_dev)
    picks = (levels[:, None] == jnp.arange(noise_table.shape[0], dtype=jnp.int32)[None, :]).astype(
        jnp.float32
    )
    gates = jnp.dot(picks, noise_table, precision=lax.Precision.HIGHEST)
    return (summed * gates[:, None, :]).astype(jnp.bfloat16)


def solution(mesh):
    placed = (
        P(("rep", "span"), "seq", "tp", None),
        P(("rep", "span"), "seq", "tp", None),
        P(("rep", "span"), "seq", "tp", None),
        P("tp", "seq"),
        P(None, "tp"),
        P("rep"),
    )
    return jax.shard_map(
        per_device,
        mesh=mesh,
        in_specs=placed,
        out_specs=P(("rep", "span"), "seq", "tp"),
        check_vma=False,
    )
```

profile of v0, /device:TPU:0, one launch (start us, length us, event | category | flops | bytes accessed | tf_op | source)
XLA Modules:
  0.0 320.5 jit_solution(18199733619609409647)
XLA Ops:
  6.5 1.0 copy.63
  7.5 18.0 %all_gather.15 = bf16[2,512,2,128]{3,1,2,0:T(8,128)(2,1)} all-gather(bf16[2,128,2,128]{3,1,2,0:T(8,128)(2,1)S(1)} %copy.63), channel_id=1, replica_groups=mesh['rep'=2,'span'=2,'seq'=4,'tp'=2] {'seq'}, dimensions={1}, use_global_device_ids=true | all-gather | bytes 655360 | tf_op jit(solution)/shard_map/all_gather | solution.py:38
  25.6 0.9 copy.64
  26.5 17.0 %all_gather.17 = bf16[2,512,2,128]{3,1,2,0:T(8,128)(2,1)} all-gather(bf16[2,128,2,128]{3,1,2,0:T(8,128)(2,1)S(1)} %copy.64), channel_id=1, replica_groups=mesh['rep'=2,'span'=2,'seq'=4,'tp'=2] {'seq'}, dimensions={1}, use_global_device_ids=true | all-gather | bytes 655360 | tf_op jit(solution)/shard_map/all_gather | solution.py:39
  43.7 9.6 %all-gather.6.cloned.1.call-done = bf16[4,512,2,128]{3,1,2,0:T(8,128)(2,1)} async-done(((bf16[2,512,2,128]{3,1,2,0:T(8,128)(2,1)}), bf16[4,512,2,128]{3,1,2,0:T(8,128)(2,1)}) %all-gather.6.cloned.1.call-update) | async-done | bytes 1048592 | tf_op jit(solution)/shard_map/all_gather | solution.py:42
  53.3 6.1 %conditional.12 = (f32[128,2,6]{0,2,1:T(8,128)}, f32[128,2,6]{0,2,1:T(8,128)S(1)}, f32[128,2,6,128]{3,0,2,1:T(8,128)S(1)}) conditional(s32[]{:T(128)} %convert_element_type.70, () %tuple.93, (bf16[4,512,2,128]{3,1,2,0:T(8,128)(2,1)}, bf16[2,128,2,6,128]{4,1,3,2,0:T(8,128)(2,1)}, bf16[4,512,2,128]{3,1,2,0:T(8,128)(2,1)}) %tuple.190), branch_computations={%region_16.0_spmd, %region_17.0_spmd} | conditional | flops 409147392 | bytes 11210776 | solution.py:55
  53.3 1.7 bitcast_reduce_fusion.4
  55.6 1.2 fusion.85
  56.8 0.7 fusion.104
  57.5 1.9 fusion.93
  59.4 6.2 %conditional.13 = ((f32[128,2,6]{0,2,1:T(8,128)}, f32[128,2,6]{0,2,1:T(8,128)S(1)}, f32[128,2,6,128]{3,0,2,1:T(8,128)S(1)})) conditional(s32[]{:T(128)} %convert_element_type.69, (f32[128,2,6]{0,2,1:T(8,128)}, f32[128,2,6]{0,2,1:T(8,128)S(1)}, f32[128,2,6,128]{3,0,2,1:T(8,128)S(1)}) %conditional.12, (f32[128,2,6]{0,2,1:T(8,128)}, ...), branch_computations={%region_20.0_spmd, %region_21.0_spmd} | conditional | flops 409344000 | bytes 12032032 | solution.py:55
  59.4 1.7 bitcast_reduce_fusion.5
  62.3 0.7 multiply_add_fusion.4
  63.6 2.0 fusion.115
  65.6 6.1 %conditional.8 = (f32[128,2,6]{0,2,1:T(8,128)}, f32[128,2,6]{0,2,1:T(8,128)S(1)}, f32[128,2,6,128]{3,0,2,1:T(8,128)S(1)}) conditional(s32[]{:T(128)} %convert_element_type.66, () %tuple.87, (bf16[4,512,2,128]{3,1,2,0:T(8,128)(2,1)}, bf16[2,128,2,6,128]{4,1,3,2,0:T(8,128)(2,1)}, bf16[4,512,2,128]{3,1,2,0:T(8,128)(2,1)}) %tuple.193), branch_computations={%region_0.0_spmd, %region_1.0_spmd} | conditional | flops 409147392 | bytes 11210776 | solution.py:55
  65.6 1.7 bitcast_reduce_fusion
  67.9 1.2 fusion.2
  69.8 1.9 fusion.10
  72.0 1.5 conditional.15
  72.2 1.2 copy.102
  73.4 1.4 conditional.11
  73.7 1.2 copy.100
  75.0 1.6 copy.73
  76.6 2.9 fusion.171
  79.6 93.0 %all-gather.8.cloned.1.call-done = bf16[2,512,1536]{2,1,0:T(8,128)(2,1)} async-done(((bf16[2,128,1536]{2,1,0:T(8,128)(2,1)}), bf16[2,512,1536]{2,1,0:T(8,128)(2,1)}) %all-gather.8.cloned.1.call-update) | async-done | bytes 3145744 | tf_op jit(solution)/shard_map/all_gather | solution.py:68
  172.6 8.1 %fusion.168 = bf16[2,512,1536]{2,1,0:T(8,128)(2,1)S(1)} fusion(bf16[2,512,1536]{2,1,0:T(8,128)(2,1)} %all-gather.8.cloned.1.call-done, bf16[1536,1536]{1,0:T(8,128)(2,1)} %param.25), kind=kOutput, calls=%fused_computation.166 | convolution fusion | flops 4833411072 | bytes 11010048 | tf_op jit(solution)/shard_map/ctf,fo->cto/dot_general | solution.py:66
  180.7 3.2 %copy.74 = bf16[2,512,1536]{2,0,1:T(2,128)(2,1)S(1)} copy(bf16[2,512,1536]{2,1,0:T(8,128)(2,1)S(1)} %fusion.168) | data formatting | bytes 6291456 | tf_op jit(solution)/shard_map/convert_element_type | solution.py:73
  183.9 73.3 %all_to_all.18 = bf16[2,512,1536]{2,0,1:T(2,128)(2,1)S(1)} all-to-all(bf16[2,512,1536]{2,0,1:T(2,128)(2,1)S(1)} %copy.74), channel_id=1, replica_groups=mesh['rep'=2,'span'=2,'seq'=4,'tp'=2] {'seq'}, dimensions={1} | all-to-all | bytes 6291456 | tf_op jit(solution)/shard_map/all_to_all | solution.py:72
  257.2 4.1 %copy.75 = bf16[2,128,4,1536]{3,2,1,0:T(4,128)(2,1)} copy(bf16[2,128,4,1536]{3,0,1,2:T(2,128)(2,1)S(1)} %bitcast.326) | data formatting | bytes 6291456 | tf_op jit(solution)/shard_map/all_to_all | solution.py:72
  261.3 6.9 %all_to_all.16 = bf16[2,128,6144]{2,1,0:T(8,128)(2,1)} reshape(bf16[2,128,4,1536]{3,2,1,0:T(4,128)(2,1)} %copy.75) | data formatting | bytes 6291456 | tf_op jit(solution)/shard_map/all_to_all | solution.py:72
  269.4 41.7 %reduce-scatter.2.cloned.1.call-done = bf16[2,128,3072]{2,1,0:T(8,128)(2,1)} async-done(((bf16[2,128,6144]{2,1,0:T(8,128)(2,1)}), bf16[2,128,3072]{2,1,0:T(8,128)(2,1)}) %reduce-scatter.2.cloned.1.call-update) | async-done | bytes 1572880 | tf_op jit(solution)/shard_map/reduce_scatter | solution.py:75
  311.1 2.9 multiply_convert_fusion
  (28 shorter events, 5.9 us)
Async XLA Ops:
  6.5 262.4 %copy-start = (f32[64,3072]{1,0:T(8,128)S(1)}, f32[64,3072]{1,0:T(8,128)}, u32[]{:S(2)}) copy-start(f32[64,3072]{1,0:T(8,128)} %param.26) | copy-start | bytes 2359300
  6.5 37.2 %all-gather.4.cloned.1.call-start = ((), (), s32[]{:S(2)}) async-start(), calls=%async_computation.2 | async-start | bytes 1572864 | tf_op jit(solution)/shard_map/all_gather | solution.py:41
  25.6 27.7 %all-gather.6.cloned.1.call-start = ((), (), s32[]{:S(2)}) async-start(), calls=%async_computation.3 | async-start | bytes 1572864 | tf_op jit(solution)/shard_map/all_gather | solution.py:42
  43.6 129.0 %all-gather.8.cloned.1.call-start = ((), (), s32[]{:S(2)}) async-start(), calls=%async_computation.4 | async-start | bytes 3932160 | tf_op jit(solution)/shard_map/all_gather | solution.py:68
  79.6 231.5 %reduce-scatter.2.cloned.1.call-start = ((), (), s32[]{:S(2)}) async-start(), calls=%async_computation.5 | async-start | bytes 4718592 | tf_op jit(solution)/shard_map/reduce_scatter | solution.py:75
  268.3 0.7 copy-start.5
Sparse Core Ops, SparseCore 0:
  25.7 10.8 all-gather.3
  43.7 9.5 all-gather.5
  79.7 92.8 all-gather.7
  268.4 42.6 reduce-scatter.1
where the time goes:
time: 322 us; the launch traced here: 321 us
  waiting for transfers between devices  144 us (45%)
  blocking collectives  108 us (34%)
  local copies, waits for them, and re-layouts  22.1 us (7%)
  matrix products  19.2 us (6%)
  between operations  13.2 us (4%)
  other arithmetic  12.9 us (4%)
    all_gather x1, waiting for transfers between devices, per_device(): lax.all_gather(attn, 'seq', axis=1, tiled=True)  93 us
    all_to_all x1, blocking collectives, per_device(): lax.all_to_all(columns.astype(jnp.bfloat16), 'seq', split_axis=1, concat_...  73.3 us
    reduce_scatter x1, waiting for transfers between devices, per_device(): lax.psum_scatter(partial_out.astype(jnp.bfloat16), 'tp', scatter_dimensio...  41.7 us
    all_gather x1, blocking collectives, per_device(): lax.all_gather(key_states, 'seq', axis=1, tiled=True)  18 us
    all_gather x1, blocking collectives, per_device(): lax.all_gather(value_states, 'seq', axis=1, tiled=True)  17 us
    all_to_all x2, local copies, waits for them, and re-layouts, per_device(): lax.all_to_all(columns.astype(jnp.bfloat16), 'seq', split_axis=1, concat_...  11 us
    all_gather x1, waiting for transfers between devices, per_device(): value_piece = lax.all_gather(span_rows[1], 'span', axis=0, tiled=True)  9.6 us
    dot_general x1, matrix products, per_device(): jnp.einsum('ctf,fo->cto', lax.all_gather(attn, 'seq', axis=1, tiled=True)...  8.06 us
  transfers between devices with their start and end apart: 4, of which 3 were waited for; matrix products, arithmetic and copies ran while one was open for 0% of the time, Pallas kernels for 0%

commit v1 on v0

--- a/solution.py
+++ b/solution.py
@@ -2,6 +2,12 @@
 import jax.numpy as jnp
 from jax import lax
 from jax.sharding import PartitionSpec as P
+
+
+def in_order(blocks, dim):
+    blocks = jnp.moveaxis(blocks, 0, dim)
+    shape = blocks.shape
+    return blocks.reshape(*shape[:dim], shape[dim] * shape[dim + 1], *shape[dim + 2 :])
 
 
 def fold_block(carried, query_rows, key_rows, value_rows, factor):
@@ -63,12 +69,18 @@
         .reshape(ch_dev, tok_dev, heads_local * head_size)
         .astype(jnp.bfloat16)
     )
-    columns = jnp.einsum(
-        "ctf,fo->cto",
-        lax.all_gather(attn, "seq", axis=1, tiled=True),
-        out_weight,
-        preferred_element_type=jnp.float32,
-    )
+    devices, mine, extent = (lax.axis_size("seq"), lax.axis_index("seq"), attn.shape[1])
+    upward = [(i, (i + 1) % devices) for i in range(devices)]
+    blocks = []
+    current = attn
+    for step in range(devices):
+        coming = current if step == devices - 1 else lax.ppermute(current, "seq", upward)
+        blocks.append(
+            jnp.einsum("ctf,fo->cto", current, out_weight, preferred_element_type=jnp.float32)
+        )
+        current = coming
+    blocks = jnp.stack(blocks)[(mine - jnp.arange(devices)) % devices]
+    columns = in_order(blocks, 1)
     partial_out = lax.all_to_all(
         columns.astype(jnp.bfloat16), "seq", split_axis=1, concat_axis=2, tiled=True
     ).astype(columns.dtype)

time: 322 us -> 281 us (0.87)
  waiting for transfers between devices: 144 us -> 96 us
  local copies, waits for them, and re-layouts: 22.1 us -> 26 us
  matrix products: 19.2 us -> 22.6 us
    all_gather x1 -> x0, waiting for transfers between devices: 93 us -> none  [per_device(): lax.all_gather(attn, 'seq', axis=1, tiled=True)]
    ppermute x0 -> x3, waiting for transfers between devices: none -> 38 us  [per_device(): lax.ppermute(current, 'seq', upward)]
    reduce_scatter x1, waiting for transfers between devices: 41.7 us -> 48.3 us  [per_device(): lax.psum_scatter(partial_out.astype(jnp.bfloat16), 'tp', scatter_dimensio...]
    gather x0 -> x1, local copies, waits for them, and re-layouts: none -> 4.32 us  [per_device(): blocks = jnp.stack(blocks)[(mine - jnp.arange(devices)) % devices]]
    all_to_all x2, local copies, waits for them, and re-layouts: 11 us -> 6.8 us  [per_device(): lax.all_to_all(columns.astype(jnp.bfloat16), 'seq', split_axis=1, concat_...]
    dot_general x1 -> x4, matrix products: 8.06 us -> 11.5 us  [per_device(): jnp.einsum('ctf,fo->cto', current, out_weight, preferred_element_type=jnp...]
  transfers between devices with their start and end apart: 4 -> 6, of which waited for: 3 -> 5; matrix products, arithmetic and copies ran while one was open for 0% -> 4% of each run, Pallas kernels for 0% -> 0%
where the time goes in v1:
time: 281 us; the launch traced here: 280 us
  blocking collectives  107 us (38%)
  waiting for transfers between devices  96 us (34%)
  local copies, waits for them, and re-layouts  26 us (9%)
  matrix products  22.6 us (8%)
  between operations  13.3 us (5%)
  other arithmetic  13.1 us (5%)
    all_to_all x1, blocking collectives, per_device(): lax.all_to_all(columns.astype(jnp.bfloat16), 'seq', split_axis=1, concat_...  72 us
    reduce_scatter x1, waiting for transfers between devices, per_device(): lax.psum_scatter(partial_out.astype(jnp.bfloat16), 'tp', scatter_dimensio...  48.3 us
    ppermute x3, waiting for transfers between devices, per_device(): lax.ppermute(current, 'seq', upward)  38 us
    all_gather x1, blocking collectives, per_device(): lax.all_gather(key_states, 'seq', axis=1, tiled=True)  18 us
    all_gather x1, blocking collectives, per_device(): lax.all_gather(value_states, 'seq', axis=1, tiled=True)  17 us
    dot_general x4, matrix products, per_device(): jnp.einsum('ctf,fo->cto', current, out_weight, preferred_element_type=jnp...  11.5 us
    all_gather x1, waiting for transfers between devices, per_device(): value_piece = lax.all_gather(span_rows[1], 'span', axis=0, tiled=True)  9.6 us
    all_to_all x2, local copies, waits for them, and re-layouts, per_device(): lax.all_to_all(columns.astype(jnp.bfloat16), 'seq', split_axis=1, concat_...  6.8 us
  transfers between devices with their start and end apart: 6, of which 5 were waited for; matrix products, arithmetic and copies ran while one was open for 4% of the time, Pallas kernels for 0%

profile of v1, /device:TPU:0, one launch (start us, length us, event | category | flops | bytes accessed | tf_op | source)
XLA Modules:
  0.0 280.1 jit_solution(11749001129661108314)
XLA Ops:
  7.5 18.0 %all_gather.12 = bf16[2,512,2,128]{3,1,2,0:T(8,128)(2,1)} all-gather(bf16[2,128,2,128]{3,1,2,0:T(8,128)(2,1)S(1)} %copy.88), channel_id=1, replica_groups=mesh['rep'=2,'span'=2,'seq'=4,'tp'=2] {'seq'}, dimensions={1}, use_global_device_ids=true | all-gather | bytes 655360 | tf_op jit(solution)/shard_map/all_gather | solution.py:44
  26.5 17.0 %all_gather.14 = bf16[2,512,2,128]{3,1,2,0:T(8,128)(2,1)} all-gather(bf16[2,128,2,128]{3,1,2,0:T(8,128)(2,1)S(1)} %copy.89), channel_id=1, replica_groups=mesh['rep'=2,'span'=2,'seq'=4,'tp'=2] {'seq'}, dimensions={1}, use_global_device_ids=true | all-gather | bytes 655360 | tf_op jit(solution)/shard_map/all_gather | solution.py:45
  43.7 9.6 %all-gather.5.cloned.1.call-done = bf16[4,512,2,128]{3,1,2,0:T(8,128)(2,1)} async-done(((bf16[2,512,2,128]{3,1,2,0:T(8,128)(2,1)}), bf16[4,512,2,128]{3,1,2,0:T(8,128)(2,1)}) %all-gather.5.cloned.1.call-update) | async-done | bytes 1048592 | tf_op jit(solution)/shard_map/all_gather | solution.py:48
  53.3 6.1 %conditional.12 = (f32[128,2,6]{0,2,1:T(8,128)}, f32[128,2,6]{0,2,1:T(8,128)S(1)}, f32[128,2,6,128]{3,0,2,1:T(8,128)S(1)}) conditional(s32[]{:T(128)} %convert_element_type.76, () %tuple.93, (bf16[4,512,2,128]{3,1,2,0:T(8,128)(2,1)}, bf16[2,128,2,6,128]{4,1,3,2,0:T(8,128)(2,1)}, bf16[4,512,2,128]{3,1,2,0:T(8,128)(2,1)}) %tuple.198), branch_computations={%region_16.0_spmd, %region_17.0_spmd} | conditional | flops 409147392 | bytes 11210776 | solution.py:61
  53.3 1.7 bitcast_reduce_fusion.4
  57.5 1.9 fusion.93
  59.4 6.2 %conditional.13 = ((f32[128,2,6]{0,2,1:T(8,128)}, f32[128,2,6]{0,2,1:T(8,128)S(1)}, f32[128,2,6,128]{3,0,2,1:T(8,128)S(1)})) conditional(s32[]{:T(128)} %convert_element_type.75, (f32[128,2,6]{0,2,1:T(8,128)}, f32[128,2,6]{0,2,1:T(8,128)S(1)}, f32[128,2,6,128]{3,0,2,1:T(8,128)S(1)}) %conditional.12, (f32[128,2,6]{0,2,1:T(8,128)}, ...), branch_computations={%region_20.0_spmd, %region_21.0_spmd} | conditional | flops 409344000 | bytes 12032032 | solution.py:61
  59.4 1.7 bitcast_reduce_fusion.5
  63.6 2.0 fusion.115
  65.6 6.1 %conditional.8 = (f32[128,2,6]{0,2,1:T(8,128)}, f32[128,2,6]{0,2,1:T(8,128)S(1)}, f32[128,2,6,128]{3,0,2,1:T(8,128)S(1)}) conditional(s32[]{:T(128)} %convert_element_type.72, () %tuple.87, (bf16[4,512,2,128]{3,1,2,0:T(8,128)(2,1)}, bf16[2,128,2,6,128]{4,1,3,2,0:T(8,128)(2,1)}, bf16[4,512,2,128]{3,1,2,0:T(8,128)(2,1)}) %tuple.201), branch_computations={%region_0.0_spmd, %region_1.0_spmd} | conditional | flops 409147392 | bytes 11210776 | solution.py:61
  65.6 1.7 bitcast_reduce_fusion
  69.8 1.9 fusion.10
  72.0 1.5 conditional.15
  75.0 1.6 copy.98
  76.6 2.1 fusion.186
  78.7 1.8 collective-permute-start
  80.5 12.0 %collective-permute-done = bf16[2,128,1536]{2,1,0:T(8,128)(2,1)S(1)} collective-permute-done((bf16[2,128,1536]{2,1,0:T(8,128)(2,1)S(1)}, bf16[2,128,1536]{2,1,0:T(8,128)(2,1)S(1)}, u32[]{:S(2)}, u32[]{:S(2)}) %collective-permute-start) | collective-permute-done | bytes 786464 | tf_op jit(solution)/shard_map/ppermute | solution.py:77
  92.6 3.9 %fusion.174 = bf16[1,2,128,1536]{3,2,1,0:T(8,128)(2,1)S(1)} fusion(bf16[2,128,1536]{2,1,0:T(8,128)(2,1)S(1)} %fusion.186, bf16[1536,1536]{1,0:T(8,128)(2,1)} %param.25), kind=kOutput, calls=%fused_computation.176 | convolution fusion | flops 1207959552 | bytes 6291456 | tf_op jit(solution)/shard_map/ctf,fo->cto/dot_general | solution.py:79
  96.4 10.0 %collective-permute-done.1 = bf16[2,128,1536]{2,1,0:T(8,128)(2,1)} collective-permute-done((bf16[2,128,1536]{2,1,0:T(8,128)(2,1)S(1)}, bf16[2,128,1536]{2,1,0:T(8,128)(2,1)}, u32[]{:S(2)}, u32[]{:S(2)}) %collective-permute-start.1) | collective-permute-done | bytes 786464 | tf_op jit(solution)/shard_map/ppermute | solution.py:77
  106.4 3.7 %fusion.177 = bf16[1,2,128,1536]{3,2,1,0:T(8,128)(2,1)S(1)} fusion(bf16[2,128,1536]{2,1,0:T(8,128)(2,1)S(1)} %collective-permute-done, bf16[1536,1536]{1,0:T(8,128)(2,1)} %param.25), kind=kOutput, calls=%fused_computation.177 | convolution fusion | flops 1207959552 | bytes 6291456 | tf_op jit(solution)/shard_map/ctf,fo->cto/dot_general | solution.py:79
  110.2 2.5 fusion.180
  112.7 16.0 %collective-permute-done.2 = bf16[2,128,1536]{2,1,0:T(8,128)(2,1)S(1)} collective-permute-done((bf16[2,128,1536]{2,1,0:T(8,128)(2,1)}, bf16[2,128,1536]{2,1,0:T(8,128)(2,1)S(1)}, u32[]{:S(2)}, u32[]{:S(2)}) %collective-permute-start.2) | collective-permute-done | bytes 786464 | tf_op jit(solution)/shard_map/ppermute | solution.py:77
  130.0 1.9 pad_maximum_fusion
  131.9 4.3 %gather_fusion = bf16[4,2,128,1536]{3,2,1,0:T(8,128)(2,1)} fusion(bf16[4,2,128,1536]{3,2,1,0:T(8,128)(2,1)} %pad_maximum_fusion, s32[1024]{0:T(1024)S(1)} %pad_clamp_fusion), kind=kCustom, calls=%fused_computation | custom fusion | bytes 6291472 | tf_op jit(solution)/shard_map/gather | solution.py:82
  136.2 2.2 copy.99
  138.4 3.2 %copy.100 = bf16[2,512,1536]{2,0,1:T(2,128)(2,1)S(1)} copy(bf16[2,512,1536]{2,1,0:T(8,128)(2,1)S(1)} %bitcast.358) | data formatting | bytes 6291456 | tf_op jit(solution)/shard_map/convert_element_type | solution.py:85
  141.7 72.0 %all_to_all.18 = bf16[2,512,1536]{2,0,1:T(2,128)(2,1)S(1)} all-to-all(bf16[2,512,1536]{2,0,1:T(2,128)(2,1)S(1)} %copy.100), channel_id=1, replica_groups=mesh['rep'=2,'span'=2,'seq'=4,'tp'=2] {'seq'}, dimensions={1} | all-to-all | bytes 6291456 | tf_op jit(solution)/shard_map/all_to_all | solution.py:84
  213.7 2.2 copy.101
  215.9 4.6 %copy.102 = bf16[2,128,4,1536]{1,3,2,0:T(8,128)(2,1)} copy(bf16[2,128,4,1536]{3,1,2,0:T(8,128)(2,1)} %bitcast.359) | data formatting | bytes 6291456 | tf_op jit(solution)/shard_map/all_to_all | solution.py:84
  221.6 48.3 %reduce-scatter.2.cloned.1.call-done = bf16[2,128,3072]{1,2,0:T(8,128)(2,1)} async-done(((bf16[2,128,6144]{1,2,0:T(8,128)(2,1)}), bf16[2,128,3072]{1,2,0:T(8,128)(2,1)}) %reduce-scatter.2.cloned.1.call-update) | async-done | bytes 1572880 | tf_op jit(solution)/shard_map/reduce_scatter | solution.py:87
  269.9 2.1 multiply_convert_fusion
  272.0 1.6 copy.103
  (45 shorter events, 16.8 us)
Async XLA Ops:
  6.5 214.7 %copy-start = (f32[64,3072]{1,0:T(8,128)S(1)}, f32[64,3072]{1,0:T(8,128)}, u32[]{:S(2)}) copy-start(f32[64,3072]{1,0:T(8,128)} %param.26) | copy-start | bytes 2359300
  6.5 37.2 %all-gather.3.cloned.1.call-start = ((), (), s32[]{:S(2)}) async-start(), calls=%async_computation.2 | async-start | bytes 1572864 | tf_op jit(solution)/shard_map/all_gather | solution.py:47
  25.6 27.7 %all-gather.5.cloned.1.call-start = ((), (), s32[]{:S(2)}) async-start(), calls=%async_computation.3 | async-start | bytes 1572864 | tf_op jit(solution)/shard_map/all_gather | solution.py:48
  43.6 226.3 %reduce-scatter.2.cloned.1.call-start = ((), (), s32[]{:S(2)}) async-start(), calls=%async_computation.4 | async-start | bytes 4718592 | tf_op jit(solution)/shard_map/reduce_scatter | solution.py:87
  78.7 13.8 %collective-permute-start = (bf16[2,128,1536]{2,1,0:T(8,128)(2,1)S(1)}, bf16[2,128,1536]{2,1,0:T(8,128)(2,1)S(1)}, u32[]{:S(2)}, u32[]{:S(2)}) collective-permute-start(bf16[2,128,1536]{2,1,0:T(8,128)(2,1)S(1)} %fusion.186), channel_id=1, source_target_pairs={{0,2},{2,4},{4,6},{6,0},{1,3},{3,5},{5,7},{7,1},{8,10},{10,12},{12... | collective-permute-start | bytes 2359304 | tf_op jit(solution)/shard_map/ppermute | solution.py:77
  92.5 13.9 %collective-permute-start.1 = (bf16[2,128,1536]{2,1,0:T(8,128)(2,1)S(1)}, bf16[2,128,1536]{2,1,0:T(8,128)(2,1)}, u32[]{:S(2)}, u32[]{:S(2)}) collective-permute-start(bf16[2,128,1536]{2,1,0:T(8,128)(2,1)S(1)} %collective-permute-done), channel_id=1, source_target_pairs={{0,2},{2,4},{4,6},{6,0},{1,3},{3,5},{5,7},{7,1},{8,10},{10,12},{12... | collective-permute-start | bytes 2359304 | tf_op jit(solution)/shard_map/ppermute | solution.py:77
  92.5 17.6 %slice-start = ((s8[4718592]{0:T(1024)(128)(4,1)}), s8[4194304]{0:T(1024)(128)(4,1)S(1)}, s32[]{:S(2)}) async-start(s8[4718592]{0:T(1024)(128)(4,1)} %bitcast.367), calls=%async_computation.5 | async-start | bytes 8388608
  92.5 17.6 %slice-start.1 = ((s8[4718592]{0:T(1024)(128)(4,1)}), s8[524288]{0:T(1024)(128)(4,1)S(1)}, s32[]{:S(2)}) async-start(s8[4718592]{0:T(1024)(128)(4,1)} %bitcast.367), calls=%async_computation.6 | async-start | bytes 1048576
  106.4 22.3 %collective-permute-start.2 = (bf16[2,128,1536]{2,1,0:T(8,128)(2,1)}, bf16[2,128,1536]{2,1,0:T(8,128)(2,1)S(1)}, u32[]{:S(2)}, u32[]{:S(2)}) collective-permute-start(bf16[2,128,1536]{2,1,0:T(8,128)(2,1)} %collective-permute-done.1), channel_id=1, source_target_pairs={{0,2},{2,4},{4,6},{6,0},{1,3},{3,5},{5,7},{7,1},{8,10},{10,12},{12... | collective-permute-start | bytes 2359304 | tf_op jit(solution)/shard_map/ppermute | solution.py:77
  220.5 0.7 copy-start.5
Sparse Core Ops, SparseCore 0:
  25.7 10.8 all-gather.2
  43.7 9.5 all-gather.4
  220.6 49.2 reduce-scatter.1
